TPU v7x, 16 devices: a whole 2x2x2 slice. The times are simulated.
16 devices in a mesh: rep: 1, dp: 16 (over x, y, z, core).
Axes of the slice: x: 2, y: 2, z: 2, core: 2. Of those that a mesh axis runs over, the one named last changes fastest.
Arguments:
- x: bfloat16 [16, 2048, 512], P(('rep', 'dp'))
- dy: bfloat16 [16, 2048, 512], P(('rep', 'dp'))
- w_gate: bfloat16 [2, 512, 4096], replicated
- w_up: bfloat16 [2, 512, 4096], replicated
- w_down: bfloat16 [2, 4096, 512], replicated
- m_w_gate: float32 [2, 512, 4096], replicated
- m_w_up: float32 [2, 512, 4096], replicated
- m_w_down: float32 [2, 4096, 512], replicated
- v_w_gate: float32 [2, 512, 4096], replicated
- v_w_up: float32 [2, 512, 4096], replicated
- v_w_down: float32 [2, 4096, 512], replicated
Outputs:
- output 1: bfloat16 [2, 512, 4096], P('rep')
- output 2: bfloat16 [2, 512, 4096], P('rep')
- output 3: bfloat16 [2, 4096, 512], P('rep')
- output 4: float32 [2, 512, 4096], P('rep')
- output 5: float32 [2, 512, 4096], P('rep')
- output 6: float32 [2, 4096, 512], P('rep')
- output 7: float32 [2, 512, 4096], P('rep')
- output 8: float32 [2, 512, 4096], P('rep')
- output 9: float32 [2, 4096, 512], P('rep')
All inputs are finite; a program needn't handle non-finite values.
Results may differ from a plain program's by a relative error of at most 0.022.
Values are sent between devices in bfloat16 or wider.
A program may use at most 2.5 GiB of HBM per device.

v0:
```python
import jax
import jax.numpy as jnp
from jax import lax
from jax.sharding import PartitionSpec as P

NAMES = ("w_gate", "w_up", "w_down")


def matmul(a, w):
    return jnp.dot(a, w, preferred_element_type=jnp.float32).astype(jnp.bfloat16)


def normed(h):
    wide = h.astype(jnp.float32)
    scale = lax.rsqrt(jnp.mean(wide**2, -1, keepdims=True) + 1e-6)
    return (wide * scale).astype(jnp.bfloat16)


def layer(h, w):
    a = normed(h)
    gate = jnp.dot(a, w["w_gate"], preferred_element_type=jnp.float32)
    up = jnp.dot(a, w["w_up"], preferred_element_type=jnp.float32)
    return h + matmul((jax.nn.silu(gate) * up).astype(jnp.bfloat16), w["w_down"])


def adamw(w, m, v, g):
    m = 0.9 * m + 0.1 * g
    v = 0.95 * v + 0.05 * g * g
    step = m * lax.rsqrt(v + 1e-8) + 0.1 * w
    return (w - 0.02 * step).astype(jnp.bfloat16), m, v


def clipped(gradients, sum_of_squares, count):
    factor = jnp.minimum(1.0, 0.5 * lax.rsqrt(sum_of_squares / count + 1e-30))
    return [g * factor for g in gradients]


def solution(mesh):
    def step(x, dy, *arrays):
        weights, m, v = (arrays[i : i + 3] for i in (0, 3, 6))
        layers = weights[0].shape[0]
        h, kept = x[0], []
        for number in range(layers):
            kept.append(h)
            h = layer(h, {name: w[number] for name, w in zip(NAMES, weights, strict=True)})
        by_h, summed = dy[0], [None] * layers
        for number in reversed(range(layers)):
            _, back = jax.vjp(lambda w, h: layer(h, w), {name: w[number] for name, w in zip(NAMES, weights, strict=True)}, kept[number])
            by_w, by_h = back(by_h)
            summed[number] = [lax.psum(by_w[name], "dp") for name in NAMES]
        gradients = [jnp.stack([summed[number][i] for number in range(layers)]).astype(jnp.float32) for i in range(3)]
        gradients = clipped(gradients, sum(jnp.sum(g * g) for g in gradients), sum(g.size for g in gradients))
        new = [adamw(w.astype(jnp.float32), m, v, g) for w, m, v, g in zip(weights, m, v, gradients, strict=True)]
        return tuple(one[which] for which in range(3) for one in new)

    return jax.shard_map(
        step,
        mesh=mesh,
        in_specs=(P(("rep", "dp"), None, None),) * 2 + (P(None, None, None),) * 9,
        out_specs=(P("rep", None, None),) * 9,
        check_vma=False,
    )
```

profile of v0, /device:TPU:0, one launch (start us, length us, event | category | flops | bytes accessed | tf_op | source)
XLA Modules:
  0.0 702.4 jit_solution(15070527175715975274)
XLA Ops:
  7.2 2.9 copy.20
  10.6 4.2 copy.21
  14.8 15.2 %convolution_convert_fusion.1 = bf16[2048,4096]{1,0:T(8,128)(2,1)} fusion(bf16[2,4096,512]{2,1,0:T(8,128)(2,1)} %param.15, bf16[1,2048,512]{2,1,0:T(8,128)(2,1)} %param.12), kind=kOutput, calls=%fused_computation.61 | convolution fusion | flops 8598323200 | bytes 23068672 | tf_op jit(solution)/shard_map/transpose(jvp())/dot_general | solution.py:10
  30.0 16.9 %fusion.71 = f32[2048,4096]{1,0:T(8,128)} fusion(bf16[2,512,4096]{2,1,0:T(8,128)(2,1)} %param.13, bf16[1,2048,512]{2,1,0:T(8,128)(2,1)S(1)} %copy-done.7, f32[2048]{0:T(1024)S(1)} %add_rsqrt_fusion), kind=kOutput, calls=%fused_computation.104 | convolution fusion | flops 8593080320 | bytes 39854080 | tf_op jit(solution)/shard_map/dot_general | solution.py:21
  46.9 32.7 %multiply_convert_fusion.1 = (bf16[2048,4096]{1,0:T(8,128)(2,1)}, f32[2048,4096]{1,0:T(8,128)}) fusion(f32[2048,4096]{1,0:T(8,128)} %fusion.71, bf16[2,512,4096]{2,1,0:T(8,128)(2,1)} %param.14, bf16[1,2048,512]{2,1,0:T(8,128)(2,1)} %param.11, f32[2048]{0:T(1024)S(1)} %add_rsqrt_fusion), kind=kOutput, calls=%fused_computation.17 | convolution fusion | flops 8643411968 | bytes 90185728 | tf_op jit(solution)/shard_map/dot_general | solution.py:22
  79.6 15.0 %fusion.55 = (f32[2048]{0:T(1024)S(1)}, bf16[2048,512]{0,1:T(8,128)(2,1)}) fusion(bf16[2048,4096]{1,0:T(8,128)(2,1)} %get-tuple-element.24, bf16[2,4096,512]{2,1,0:T(8,128)(2,1)} %param.15, bf16[1,2048,512]{1,2,0:T(8,128)(2,1)S(1)} %copy.20), kind=kOutput, calls=%fused_computation.88 | convolution fusion | flops 8595175424 | bytes 25174016 | tf_op jit(solution)/shard_map/dot_general | solution.py:10
  94.7 18.0 %fusion.58 = f32[2048,4096]{1,0:T(8,128)} fusion(bf16[2,512,4096]{2,1,0:T(8,128)(2,1)} %param.14, bf16[2048,512]{0,1:T(8,128)(2,1)} %get-tuple-element.27, f32[2048]{0:T(1024)S(1)} %fusion.109), kind=kOutput, calls=%fused_computation.91 | convolution fusion | flops 8593080320 | bytes 39854080 | tf_op jit(solution)/shard_map/jvp()/dot_general | solution.py:22
  112.7 39.7 %fusion.2 = (bf16[2048,4096]{1,0:T(8,128)(2,1)}, f32[2048,4096]{1,0:T(8,128)}) fusion(f32[2048,4096]{1,0:T(8,128)} %fusion.58, bf16[2048,4096]{1,0:T(8,128)(2,1)} %convolution_convert_fusion.1, bf16[2,512,4096]{2,1,0:T(8,128)(2,1)} %param.13, bf16[2048,512]{0,1:T(8,128)(2,1)S(1)} %copy-done.9, f32[2048]{0:T(1024)S(1)} %fusion.109), kind=kOutput, calls=%fused_computation.8 | convolution fusion | flops 8693743616 | bytes 106962944 | tf_op jit(solution)/shard_map/jvp()/dot_general | solution.py:21
  152.3 20.7 %fusion.88 = bf16[2048,512]{0,1:T(8,128)(2,1)} fusion(bf16[2,512,4096]{2,1,0:T(8,128)(2,1)} %param.14, bf16[2048,4096]{1,0:T(8,128)(2,1)} %convolution_convert_fusion.1, f32[2048,4096]{1,0:T(8,128)} %get-tuple-element.29), kind=kOutput, calls=%fused_computation.118 | convolution fusion | flops 8641314816 | bytes 56623104 | tf_op jit(solution)/shard_map/transpose(jvp())/dot_general | solution.py:22
  173.0 26.1 %fusion.44 = bf16[1,4096,512]{2,1,0:T(8,128)(2,1)} fusion(f32[2048,4096]{1,0:T(8,128)} %fusion.58, bf16[1,2048,512]{2,1,0:T(8,128)(2,1)S(1)} %copy-done.8, f32[2048,4096]{1,0:T(8,128)} %get-tuple-element.29), kind=kOutput, calls=%fused_computation.76 | convolution fusion | flops 8642363392 | bytes 73400320 | tf_op jit(solution)/shard_map/transpose(jvp())/dot_general | solution.py:10
  199.0 15.2 %fusion.57 = (f32[2048]{0:T(1024)S(1)}, bf16[2048,512]{0,1:T(8,128)(2,1)S(1)}) fusion(bf16[2048,512]{0,1:T(8,128)(2,1)} %get-tuple-element.27, bf16[2048,512]{0,1:T(8,128)(2,1)} %fusion.88, bf16[2048,4096]{1,0:T(8,128)(2,1)} %get-tuple-element.28, bf16[2,512,4096]{2,1,0:T(8,128)(2,1)} %param.13), kind=kOutput, calls=%fused_computation.90 | convolution fusion | flops 8595175424 | bytes 27271168 | tf_op jit(solution)/shard_map/transpose(jvp())/dot_general | solution.py:21
  214.3 1.4 fusion.98
  215.7 14.0 %fusion.45 = bf16[1,4096,512]{2,1,0:T(8,128)(2,1)} fusion(bf16[2048,4096]{1,0:T(8,128)(2,1)} %get-tuple-element.24, bf16[2048,512]{0,1:T(8,128)(2,1)S(1)} %fusion.98), kind=kOutput, calls=%fused_computation.77 | convolution fusion | flops 8592031744 | bytes 23068672 | tf_op jit(solution)/shard_map/transpose(jvp())/dot_general | solution.py:10
  229.7 15.0 %convolution_convert_fusion = bf16[2048,4096]{1,0:T(8,128)(2,1)} fusion(bf16[2048,512]{0,1:T(8,128)(2,1)S(1)} %fusion.98, bf16[2,4096,512]{2,1,0:T(8,128)(2,1)} %param.15), kind=kOutput, calls=%fused_computation.60 | convolution fusion | flops 8598323200 | bytes 23068672 | tf_op jit(solution)/shard_map/transpose(jvp())/dot_general | solution.py:10
  244.6 21.6 %fusion.46 = bf16[1,512,4096]{2,1,0:T(8,128)(2,1)} fusion(bf16[2048,4096]{1,0:T(8,128)(2,1)} %convolution_convert_fusion.1, bf16[2048,512]{0,1:T(8,128)(2,1)S(1)} %copy-done.10, f32[2048]{0:T(1024)S(1)} %copy-done.14, f32[2048,4096]{1,0:T(8,128)} %get-tuple-element.29), kind=kOutput, calls=%fused_computation.78 | convolution fusion | flops 8645509120 | bytes 56631296 | tf_op jit(solution)/shard_map/transpose(jvp())/dot_general | solution.py:22
  266.2 13.9 %fusion.43 = bf16[1,512,4096]{2,1,0:T(8,128)(2,1)} fusion(bf16[2048,4096]{1,0:T(8,128)(2,1)} %get-tuple-element.28, bf16[2048,512]{0,1:T(8,128)(2,1)S(1)} %copy-done.10, f32[2048]{0:T(1024)S(1)} %copy-done.14), kind=kOutput, calls=%fused_computation.75 | convolution fusion | flops 8593080320 | bytes 23076864 | tf_op jit(solution)/shard_map/transpose(jvp())/dot_general | solution.py:21
  280.1 22.0 %fusion.47 = bf16[1,512,4096]{2,1,0:T(8,128)(2,1)} fusion(bf16[2048,4096]{1,0:T(8,128)(2,1)} %convolution_convert_fusion, f32[2048,4096]{1,0:T(8,128)} %fusion.71, bf16[1,2048,512]{1,2,0:T(8,128)(2,1)S(1)} %copy-done.5, f32[2048]{0:T(1024)S(1)} %copy-done.16), kind=kOutput, calls=%fused_computation.79 | convolution fusion | flops 8645509120 | bytes 56631296 | tf_op jit(solution)/shard_map/transpose(jvp())/dot_general | solution.py:22
  302.1 32.2 %fusion.48 = bf16[1,512,4096]{2,1,0:T(8,128)(2,1)} fusion(f32[2048,4096]{1,0:T(8,128)} %fusion.71, f32[2048,4096]{1,0:T(8,128)} %get-tuple-element.25, bf16[2048,4096]{1,0:T(8,128)(2,1)} %convolution_convert_fusion, bf16[1,2048,512]{1,2,0:T(8,128)(2,1)S(1)} %copy-done.5, f32[2048]{0:T(1024)S(1)} %copy-done.16), kind=kOutput, calls=%fused_computation.80 | convolution fusion | flops 8687452160 | bytes 90185728 | tf_op jit(solution)/shard_map/transpose(jvp())/dot_general | solution.py:21
  334.3 252.6 %all-reduce.3.cloned.1.call-done = (bf16[1,512,4096]{2,1,0:T(8,128)(2,1)}, bf16[1,512,4096]{2,1,0:T(8,128)(2,1)}, bf16[1,512,4096]{2,1,0:T(8,128)(2,1)}, bf16[1,...) async-done(((bf16[1,512,4096]{2,1,0:T(8,128)(2,1)}, bf16[1,512,4096]{2,1,0:T(8,128)(2,1)}, bf16[1,512,4096]{2,1,0:T(8,128)(2,1)}, ...) | async-done | bytes 25165840 | tf_op jit(solution)/shard_map/psum | solution.py:50
  586.9 7.8 %fusion.24 = f32[]{:T(128)} fusion(bf16[1,4096,512]{2,1,0:T(8,128)(2,1)} %get-tuple-element.13, bf16[1,4096,512]{2,1,0:T(8,128)(2,1)} %get-tuple-element.14), kind=kLoop, calls=%fused_computation.48 | loop fusion | flops 16777215 | bytes 8388612 | tf_op jit(solution)/shard_map/reduce_sum | solution.py:52
  594.7 7.0 %fusion.23 = f32[]{:T(128)} fusion(bf16[1,512,4096]{2,1,0:T(8,128)(2,1)} %get-tuple-element.11, bf16[1,512,4096]{2,1,0:T(8,128)(2,1)} %get-tuple-element.12), kind=kLoop, calls=%fused_computation.47 | loop fusion | flops 16777215 | bytes 8388612 | tf_op jit(solution)/shard_map/reduce_sum | solution.py:52
  601.8 4.9 fusion.22
  608.7 30.6 %fusion.30 = (bf16[2,4096,512]{2,1,0:T(8,128)(2,1)}, f32[2,4096,512]{2,1,0:T(8,128)}, f32[2,4096,512]{2,1,0:T(8,128)}) fusion(bf16[2,4096,512]{2,1,0:T(8,128)(2,1)} %param.15, f32[]{:T(128)S(6)} %min_shard_map.3, bf16[1,4096,512]{2,1,0:T(8,128)(2,1)} %get-tuple-element.13, bf16[1,4096,512]{2,1,0:T(8,128)(2,1)} %get-tuple-element.14, ...), kind=kLoop, calls=%fused_computation.54 | loop fusion | flops 83886080 | bytes 92274688 | tf_op jit(solution)/shard_map/convert_element_type | solution.py:30
  639.4 56.0 %fusion.21 = (bf16[2,512,4096]{2,1,0:T(8,128)(2,1)}, f32[2,512,4096]{2,1,0:T(8,128)}, f32[2,512,4096]{2,1,0:T(8,128)}, bf16[2,512,4096]{2,1,0:T(8,128)(2,1)}, f3...) fusion(bf16[2,512,4096]{2,1,0:T(8,128)(2,1)} %param.13, f32[]{:T(128)S(6)} %min_shard_map.3, ...), kind=kLoop, calls=%fused_computation.45 | loop fusion | flops 167772160 | bytes 184549376 | tf_op jit(solution)/shard_map/convert_element_type | solution.py:30
  (40 shorter events, 0.6 us)
Async XLA Ops:
  7.2 579.7 %all-reduce.3.cloned.1.call-start = ((), (), s32[]{:S(2)}) async-start(), calls=%async_computation | async-start | bytes 50331648 | tf_op jit(solution)/shard_map/psum | solution.py:50
  10.2 69.5 %copy-start.4 = (bf16[1,2048,512]{1,2,0:T(8,128)(2,1)}, bf16[1,2048,512]{1,2,0:T(8,128)(2,1)S(1)}, u32[]{:S(2)}) copy-start(bf16[1,2048,512]{1,2,0:T(8,128)(2,1)S(1)} %copy.20) | copy-start | bytes 6291460
  10.6 36.3 %copy-start.15 = (f32[2048]{0:T(1024)}, f32[2048]{0:T(1024)S(1)}, u32[]{:S(2)}) copy-start(f32[2048]{0:T(1024)S(1)} %add_rsqrt_fusion) | copy-start | bytes 24580
  14.8 15.2 %copy-start.7 = (bf16[1,2048,512]{2,1,0:T(8,128)(2,1)S(1)}, bf16[1,2048,512]{2,1,0:T(8,128)(2,1)}, u32[]{:S(2)}) copy-start(bf16[1,2048,512]{2,1,0:T(8,128)(2,1)} %param.11) | copy-start | bytes 6291460
  94.7 18.0 %copy-start.11 = (f32[2048]{0:T(1024)}, f32[2048]{0:T(1024)S(1)}, u32[]{:S(2)}) copy-start(f32[2048]{0:T(1024)S(1)} %get-tuple-element.26) | copy-start | bytes 24580
  94.7 18.0 %copy-start.13 = (f32[2048]{0:T(1024)}, f32[2048]{0:T(1024)S(1)}, u32[]{:S(2)}) copy-start(f32[2048]{0:T(1024)S(1)} %fusion.109) | copy-start | bytes 24580
  94.7 18.0 %copy-start.9 = (bf16[2048,512]{0,1:T(8,128)(2,1)S(1)}, bf16[2048,512]{0,1:T(8,128)(2,1)}, u32[]{:S(2)}) copy-start(bf16[2048,512]{0,1:T(8,128)(2,1)} %get-tuple-element.27) | copy-start | bytes 6291460
  152.3 20.7 %copy-start.8 = (bf16[1,2048,512]{2,1,0:T(8,128)(2,1)S(1)}, bf16[1,2048,512]{2,1,0:T(8,128)(2,1)}, u32[]{:S(2)}) copy-start(bf16[1,2048,512]{2,1,0:T(8,128)(2,1)} %param.12) | copy-start | bytes 6291460
  199.0 15.2 %copy-start.12 = (f32[2048]{0:T(1024)S(1)}, f32[2048]{0:T(1024)}, u32[]{:S(2)}) copy-start(f32[2048]{0:T(1024)} %copy-done.11) | copy-start | bytes 24580
  199.0 15.2 %copy-start.6 = (bf16[1,2048,512]{1,2,0:T(8,128)(2,1)S(1)}, bf16[1,2048,512]{1,2,0:T(8,128)(2,1)}, u32[]{:S(2)}) copy-start(bf16[1,2048,512]{1,2,0:T(8,128)(2,1)} %copy.21) | copy-start | bytes 6291460
  199.0 15.2 %copy-start.10 = (bf16[2048,512]{0,1:T(8,128)(2,1)S(1)}, bf16[2048,512]{0,1:T(8,128)(2,1)}, u32[]{:S(2)}) copy-start(bf16[2048,512]{0,1:T(8,128)(2,1)} %get-tuple-element.27) | copy-start | bytes 6291460
  199.0 15.2 %copy-start.14 = (f32[2048]{0:T(1024)S(1)}, f32[2048]{0:T(1024)}, u32[]{:S(2)}) copy-start(f32[2048]{0:T(1024)} %copy-done.13) | copy-start | bytes 24580
  266.2 13.9 %copy-start.5 = (bf16[1,2048,512]{1,2,0:T(8,128)(2,1)S(1)}, bf16[1,2048,512]{1,2,0:T(8,128)(2,1)}, u32[]{:S(2)}) copy-start(bf16[1,2048,512]{1,2,0:T(8,128)(2,1)} %copy-done.4) | copy-start | bytes 6291460
  266.2 13.9 %copy-start.16 = (f32[2048]{0:T(1024)S(1)}, f32[2048]{0:T(1024)}, u32[]{:S(2)}) copy-start(f32[2048]{0:T(1024)} %copy-done.15) | copy-start | bytes 24580
  586.9 14.9 %copy-start = (bf16[1,512,4096]{2,1,0:T(8,128)(2,1)S(1)}, bf16[1,512,4096]{2,1,0:T(8,128)(2,1)}, u32[]{:S(2)}) copy-start(bf16[1,512,4096]{2,1,0:T(8,128)(2,1)} %get-tuple-element.9) | copy-start | bytes 12582916
  586.9 14.9 %copy-start.2 = (bf16[1,512,4096]{2,1,0:T(8,128)(2,1)S(1)}, bf16[1,512,4096]{2,1,0:T(8,128)(2,1)}, u32[]{:S(2)}) copy-start(bf16[1,512,4096]{2,1,0:T(8,128)(2,1)} %get-tuple-element.10) | copy-start | bytes 12582916
  608.7 30.7 %copy-start.1 = (bf16[1,512,4096]{2,1,0:T(8,128)(2,1)S(1)}, bf16[1,512,4096]{2,1,0:T(8,128)(2,1)}, u32[]{:S(2)}) copy-start(bf16[1,512,4096]{2,1,0:T(8,128)(2,1)} %get-tuple-element.9) | copy-start | bytes 12582916
  608.7 30.7 %copy-start.3 = (bf16[1,512,4096]{2,1,0:T(8,128)(2,1)S(1)}, bf16[1,512,4096]{2,1,0:T(8,128)(2,1)}, u32[]{:S(2)}) copy-start(bf16[1,512,4096]{2,1,0:T(8,128)(2,1)} %get-tuple-element.10) | copy-start | bytes 12582916
Sparse Core Ops, SparseCore 0:
  334.4 252.4 all-reduce.2
where the time goes:
time: 710 us; the launch traced here: 702 us
  matrix products  318 us (45%)
  waiting for transfers between devices  253 us (36%)
  other arithmetic  108 us (15%)
  between operations  16.4 us (2%)
  local copies, waits for them, and re-layouts  7.17 us (1%)
    psum x1, waiting for transfers between devices, step(): summed[number] = [lax.psum(by_w[name], 'dp') for name in NAMES]  253 us
    dot_general x5, matrix products, layer(): gate = jnp.dot(a, w['w_gate'], preferred_element_type=jnp.float32)  118 us
    dot_general x5, matrix products, layer(): up = jnp.dot(a, w['w_up'], preferred_element_type=jnp.float32)  115 us
    convert_element_type x2, other arithmetic, adamw(): return ((w - 0.02 * step).astype(jnp.bfloat16), m, v)  86.6 us
    dot_general x5, matrix products, matmul(): jnp.dot(a, w, preferred_element_type=jnp.float32).astype(jnp.bfloat16)  85.2 us
    reduce_sum x3, other arithmetic, step(): jnp.sum(g * g)  19.8 us
  transfers between devices with their start and end apart: 1, of which 1 were waited for; matrix products, arithmetic and copies ran while one was open for 0% of the time, Pallas kernels for 0%

commit v1 on v0

v1 whole, which is shorter than its diff:
```python
import functools
import jax
import jax.numpy as jnp
from jax import lax
from jax.experimental import pallas as pl
from jax.experimental.pallas import tpu as pltpu
from jax.sharding import PartitionSpec as P

F32, BF16 = jnp.float32, jnp.bfloat16
VMEM_LIMIT = 67_000_000


def dot(a, b, da, db):
    return lax.dot_general(a, b, (((da,), (db,)), ((), ())), preferred_element_type=F32)


def norm_scale(wide):
    return lax.rsqrt(jnp.mean(wide * wide, -1, keepdims=True) + 1e-6)


def sigmoid(g):
    return 1.0 / (1.0 + jnp.exp(-g))


def forward_kernel(tb, x_ref, wg_ref, wu_ref, wd_ref, gate_ref, up_ref, h_ref, a_ref, at_ref, acc_ref):
    f, last = pl.program_id(0), pl.num_programs(0) - 1
    tokens = acc_ref.shape[0]

    @pl.when(f == 0)
    def _():
        for t in range(0, tokens, tb):
            rows = pl.ds(t, tb)
            wide = x_ref[0, rows, :].astype(F32)
            a = (wide * norm_scale(wide)).astype(BF16)
            a_ref[rows, :] = a
            at_ref[:, rows] = a.T
            acc_ref[rows, :] = jnp.zeros((tb, acc_ref.shape[1]), F32)

    for t in range(0, tokens, tb):
        rows = pl.ds(t, tb)
        a = a_ref[rows, :]
        gate = dot(a, wg_ref[0], 1, 0)
        up = dot(a, wu_ref[0], 1, 0)
        gate_ref[rows, :] = gate
        up_ref[rows, :] = up
        hid = (gate * sigmoid(gate) * up).astype(BF16)
        acc_ref[rows, :] += dot(hid, wd_ref[0], 1, 0)

    @pl.when(f == last)
    def _():
        for t in range(0, tokens, tb):
            rows = pl.ds(t, tb)
            h_ref[rows, :] = (x_ref[0, rows, :].astype(F32) + acc_ref[rows, :].astype(BF16).astype(F32)).astype(BF16)


def forward(x, wg, wu, wd, fb=256, tb=512):
    _, tokens, d = x.shape
    ff = wg.shape[2]
    whole = lambda *s: pl.BlockSpec(s, lambda f: (0,) * len(s))
    return pl.pallas_call(
        functools.partial(forward_kernel, tb),
        grid=(ff // fb,),
        in_specs=[
            whole(1, tokens, d),
            pl.BlockSpec((1, d, fb), lambda f: (0, 0, f)),
            pl.BlockSpec((1, d, fb), lambda f: (0, 0, f)),
            pl.BlockSpec((1, fb, d), lambda f: (0, f, 0)),
        ],
        out_specs=[
            pl.BlockSpec((tokens, fb), lambda f: (0, f)),
            pl.BlockSpec((tokens, fb), lambda f: (0, f)),
            whole(tokens, d),
            whole(tokens, d),
            whole(d, tokens),
        ],
        out_shape=[
            jax.ShapeDtypeStruct((tokens, ff), F32),
            jax.ShapeDtypeStruct((tokens, ff), F32),
            jax.ShapeDtypeStruct((tokens, d), BF16),
            jax.ShapeDtypeStruct((tokens, d), BF16),
            jax.ShapeDtypeStruct((d, tokens), BF16),
        ],
        scratch_shapes=[pltpu.VMEM((tokens, d), F32)],
        compiler_params=pltpu.CompilerParams(vmem_limit_bytes=VMEM_LIMIT),
        cost_estimate=pl.CostEstimate(flops=6 * tokens * d * ff, bytes_accessed=9 * tokens * ff, transcendentals=0),
        name="forward",
    )(x, wg, wu, wd)


def top_kernel(tb, h_ref, dy_ref, wg_ref, wu_ref, wd_ref, dwg_ref, dwu_ref, dwd_ref, dh_ref,
               a_ref, at_ref, dyt_ref, by_gate, by_up, hid_ref, dgate_ref, dup_ref):
    f, last = pl.program_id(0), pl.num_programs(0) - 1
    tokens, d = a_ref.shape

    @pl.when(f == 0)
    def _():
        for t in range(0, tokens, tb):
            rows = pl.ds(t, tb)
            wide = h_ref[rows, :].astype(F32)
            a = (wide * norm_scale(wide)).astype(BF16)
            a_ref[rows, :] = a
            at_ref[:, rows] = a.T
            dyt_ref[:, rows] = dy_ref[0, rows, :].T
            by_gate[rows, :] = jnp.zeros((tb, d), F32)
            by_up[rows, :] = jnp.zeros((tb, d), F32)

    for t in range(0, tokens, tb):
        rows = pl.ds(t, tb)
        a = a_ref[rows, :]
        gate = dot(a, wg_ref[0], 1, 0)
        up = dot(a, wu_ref[0], 1, 0)
        dhid = dot(dy_ref[0, rows, :], wd_ref[0], 1, 1).astype(BF16).astype(F32)
        s = sigmoid(gate)
        silu = gate * s
        hid_ref[rows, :] = (silu * up).astype(BF16)
        dup = (dhid * silu).astype(BF16)
        dgate = (dhid * up * (s + silu * (1.0 - s))).astype(BF16)
        dup_ref[rows, :] = dup
        dgate_ref[rows, :] = dgate
        by_gate[rows, :] += dot(dgate, wg_ref[0], 1, 1)
        by_up[rows, :] += dot(dup, wu_ref[0], 1, 1)

    dwg_ref[...] = dot(at_ref[...], dgate_ref[...], 1, 0).astype(BF16)
    dwu_ref[...] = dot(at_ref[...], dup_ref[...], 1, 0).astype(BF16)
    dwd_ref[...] = dot(dyt_ref[...], hid_ref[...], 1, 0).T.astype(BF16)

    @pl.when(f == last)
    def _():
        for t in range(0, tokens, tb):
            rows = pl.ds(t, tb)
            wide = h_ref[rows, :].astype(F32)
            scale = norm_scale(wide)
            da = (by_gate[rows, :].astype(BF16).astype(F32) + by_up[rows, :].astype(BF16).astype(F32)).astype(BF16).astype(F32)
            dn = scale * da - wide * (scale * scale * scale * jnp.mean(da * wide, -1, keepdims=True))
            dh_ref[rows, :] = (dy_ref[0, rows, :].astype(F32) + dn.astype(BF16).astype(F32)).astype(BF16)


def top(h, dy, wg, wu, wd, fb=256, tb=512):
    tokens, d = h.shape
    ff = wg.shape[2]
    whole = lambda *s: pl.BlockSpec(s, lambda f: (0,) * len(s))
    return pl.pallas_call(
        functools.partial(top_kernel, tb),
        grid=(ff // fb,),
        in_specs=[
            whole(tokens, d),
            whole(1, tokens, d),
            pl.BlockSpec((1, d, fb), lambda f: (1, 0, f)),
            pl.BlockSpec((1, d, fb), lambda f: (1, 0, f)),
            pl.BlockSpec((1, fb, d), lambda f: (1, f, 0)),
        ],
        out_specs=[
            pl.BlockSpec((d, fb), lambda f: (0, f)),
            pl.BlockSpec((d, fb), lambda f: (0, f)),
            pl.BlockSpec((fb, d), lambda f: (f, 0)),
            whole(tokens, d),
        ],
        out_shape=[
            jax.ShapeDtypeStruct((d, ff), BF16),
            jax.ShapeDtypeStruct((d, ff), BF16),
            jax.ShapeDtypeStruct((ff, d), BF16),
            jax.ShapeDtypeStruct((tokens, d), BF16),
        ],
        scratch_shapes=[
            pltpu.VMEM((tokens, d), BF16),
            pltpu.VMEM((d, tokens), BF16),
            pltpu.VMEM((d, tokens), BF16),
            pltpu.VMEM((tokens, d), F32),
            pltpu.VMEM((tokens, d), F32),
            pltpu.VMEM((tokens, fb), BF16),
            pltpu.VMEM((tokens, fb), BF16),
            pltpu.VMEM((tokens, fb), BF16),
        ],
        compiler_params=pltpu.CompilerParams(vmem_limit_bytes=VMEM_LIMIT),
        cost_estimate=pl.CostEstimate(flops=16 * tokens * d * ff, bytes_accessed=20 * d * ff, transcendentals=0),
        name="top",
    )(h, dy, wg, wu, wd)


def bottom_kernel(tb, dh_ref, at_ref, gate_ref, up_ref, wd_ref, dwg_ref, dwu_ref, dwd_ref, dht_ref, hid_ref, dgate_ref, dup_ref):
    f = pl.program_id(0)
    tokens = dh_ref.shape[0]

    @pl.when(f == 0)
    def _():
        for t in range(0, tokens, tb):
            rows = pl.ds(t, tb)
            dht_ref[:, rows] = dh_ref[rows, :].T

    for t in range(0, tokens, tb):
        rows = pl.ds(t, tb)
        gate, up = gate_ref[rows, :], up_ref[rows, :]
        dhid = dot(dh_ref[rows, :], wd_ref[0], 1, 1).astype(BF16).astype(F32)
        s = sigmoid(gate)
        silu = gate * s
        hid_ref[rows, :] = (silu * up).astype(BF16)
        dup_ref[rows, :] = (dhid * silu).astype(BF16)
        dgate_ref[rows, :] = (dhid * up * (s + silu * (1.0 - s))).astype(BF16)

    dwg_ref[...] = dot(at_ref[...], dgate_ref[...], 1, 0).astype(BF16)
    dwu_ref[...] = dot(at_ref[...], dup_ref[...], 1, 0).astype(BF16)
    dwd_ref[...] = dot(dht_ref[...], hid_ref[...], 1, 0).T.astype(BF16)


def bottom(dh, at, gate, up, wd, fb=256, tb=512):
    tokens, d = dh.shape
    ff = wd.shape[1]
    whole = lambda *s: pl.BlockSpec(s, lambda f: (0,) * len(s))
    return pl.pallas_call(
        functools.partial(bottom_kernel, tb),
        grid=(ff // fb,),
        in_specs=[
            whole(tokens, d),
            whole(d, tokens),
            pl.BlockSpec((tokens, fb), lambda f: (0, f)),
            pl.BlockSpec((tokens, fb), lambda f: (0, f)),
            pl.BlockSpec((1, fb, d), lambda f: (0, f, 0)),
        ],
        out_specs=[
            pl.BlockSpec((d, fb), lambda f: (0, f)),
            pl.BlockSpec((d, fb), lambda f: (0, f)),
            pl.BlockSpec((fb, d), lambda f: (f, 0)),
        ],
        out_shape=[
            jax.ShapeDtypeStruct((d, ff), BF16),
            jax.ShapeDtypeStruct((d, ff), BF16),
            jax.ShapeDtypeStruct((ff, d), BF16),
        ],
        scratch_shapes=[
            pltpu.VMEM((d, tokens), BF16),
            pltpu.VMEM((tokens, fb), BF16),
            pltpu.VMEM((tokens, fb), BF16),
            pltpu.VMEM((tokens, fb), BF16),
        ],
        compiler_params=pltpu.CompilerParams(vmem_limit_bytes=VMEM_LIMIT),
        cost_estimate=pl.CostEstimate(flops=8 * tokens * d * ff, bytes_accessed=9 * tokens * ff, transcendentals=0),
        name="bottom",
    )(dh, at, gate, up, wd)


def adamw_kernel(factor_ref, *refs):
    ins, outs = refs[:12], refs[12:]
    factor = factor_ref[0, 0]
    for i in range(3):
        w, m, v, g = (ins[4 * i + j] for j in range(4))
        g = g[...].astype(F32) * factor
        m = 0.9 * m[...] + 0.1 * g
        v = 0.95 * v[...] + 0.05 * g * g
        w = w[...].astype(F32)
        w = w - 0.02 * (m * lax.rsqrt(v + 1e-8) + 0.1 * w)
        outs[i][...] = w.astype(BF16)
        outs[3 + i][...] = m
        outs[6 + i][...] = v


def adamw(factor, ws, ms, vs, gs, steps=16):
    specs = []
    for w in ws:
        layers, r, c = w.shape
        specs.append(pl.BlockSpec((1, r // steps, c), lambda l, f: (l, f, 0)))
    ins, in_specs = [], []
    for w, m, v, g, spec in zip(ws, ms, vs, gs, specs):
        ins += [w, m, v, g]
        in_specs += [spec] * 4
    shapes = [jax.ShapeDtypeStruct(w.shape, t) for t in (BF16, F32, F32) for w in ws]
    return pl.pallas_call(
        adamw_kernel,
        grid=(ws[0].shape[0], steps),
        in_specs=[pl.BlockSpec(memory_space=pltpu.SMEM)] + in_specs,
        out_specs=specs * 3,
        out_shape=shapes,
        compiler_params=pltpu.CompilerParams(vmem_limit_bytes=VMEM_LIMIT),
        cost_estimate=pl.CostEstimate(flops=20 * 3 * ws[0].size, bytes_accessed=22 * 3 * ws[0].size, transcendentals=0),
        name="adamw",
    )(factor, *ins)


def solution(mesh):
    def step(x, dy, *arrays):
        ws, ms, vs = (arrays[i : i + 3] for i in (0, 3, 6))
        gate, up, h, _, at = forward(x, *ws)
        *top_g, dh = top(h, dy, *ws)
        top_g = lax.psum(top_g, "dp")
        bottom_g = bottom(dh, at, gate, up, ws[2])
        bottom_g = lax.psum(bottom_g, "dp")
        gs = [jnp.stack(pair) for pair in zip(bottom_g, top_g)]
        total = sum(jnp.sum(g.astype(F32) ** 2) for g in gs)
        factor = jnp.minimum(1.0, 0.5 * lax.rsqrt(total / sum(g.size for g in gs) + 1e-30))
        return tuple(adamw(factor.reshape(1, 1), ws, ms, vs, gs))

    return jax.shard_map(
        step,
        mesh=mesh,
        in_specs=(P(("rep", "dp"), None, None),) * 2 + (P(None, None, None),) * 9,
        out_specs=(P("rep", None, None),) * 9,
        check_vma=False,
    )
```

time: 710 us -> 578 us (0.81); the launches traced: 702 us -> 578 us
  matrix products: 318 us -> 0 us
  Pallas kernels: 0 us -> 273 us
  other arithmetic: 108 us -> 21.2 us
  local copies, waits for them, and re-layouts: 7.17 us -> 14.7 us
    dot_general x15 -> x0, matrix products: 318 us -> none  [the longest x5 118 us: layer(): gate = jnp.dot(a, w['w_gate'], preferred_element_type=jnp.float32)]
    pallas_call x0 -> x4, Pallas kernels: none -> 273 us  [the longest x1 96.3 us: adamw(): pl.pallas_call(adamw_kernel, grid=(ws[0].shape[0], steps), in_specs=[pl.B...]
    convert_element_type x2 -> x0, other arithmetic: 86.6 us -> none  [adamw(): return ((w - 0.02 * step).astype(jnp.bfloat16), m, v)]
    reduce_sum x4 -> x3, other arithmetic: 20.2 us -> 21.2 us  [step(): total = sum((jnp.sum(g.astype(F32) ** 2) for g in gs))]
where the time goes in v1:
time: 578 us
  Pallas kernels  273 us (47%)
  waiting for transfers between devices  253 us (44%)
  other arithmetic  21.2 us (4%)
  between operations  16.1 us (3%)
  local copies, waits for them, and re-layouts  14.7 us (3%)
    psum x1, waiting for transfers between devices, step(): bottom_g = lax.psum(bottom_g, 'dp')  253 us
    pallas_call x1, Pallas kernels, adamw(): pl.pallas_call(adamw_kernel, grid=(ws[0].shape[0], steps), in_specs=[pl.B...  96.3 us
    pallas_call x1, Pallas kernels, top(): pl.pallas_call(functools.partial(top_kernel, tb), grid=(ff // fb,), in_sp...  86.3 us
    pallas_call x1, Pallas kernels, bottom(): pl.pallas_call(functools.partial(bottom_kernel, tb), grid=(ff // fb,), in...  52.5 us
    pallas_call x1, Pallas kernels, forward(): pl.pallas_call(functools.partial(forward_kernel, tb), grid=(ff // fb,), i...  38.2 us
    reduce_sum x3, other arithmetic, step(): total = sum((jnp.sum(g.astype(F32) ** 2) for g in gs))  21.2 us
  transfers between devices with their start and end apart: 1, of which 1 were waited for; matrix products, arithmetic and copies ran while one was open for 0% of the time, Pallas kernels for 0%

profile of v1, /device:TPU:0, one launch (start us, length us, event | category | flops | bytes accessed | tf_op | source)
XLA Modules:
  0.0 577.9 jit_solution(15867890302564636035)
XLA Ops:
  7.2 0.0 all-reduce.3.cloned.1.call-start
  7.2 38.2 %forward.1 = (f32[2048,4096]{1,0:T(8,128)}, f32[2048,4096]{1,0:T(8,128)}, bf16[2048,512]{1,0:T(8,128)(2,1)}, bf16[2048,512]{1,0:T(8,128)(2,1)}, bf16[512,2048]{1,0:T(8,128)(2,1)}) custom-call(bf16[1,2048,512]{2,1,0:T(8,128)(2,1)} %x_ref.1, bf16[2,512,4096]{2,1,0:T(8,128)(2,1)} %refs_0_.1, bf16[2,512,4096]{2,1,0:T(8,128)(2,1)} %refs_4_.1, ...), custom_call_target="tpu_custom_call" | custom-call | flops 25769803776 | bytes 75497472 | tf_op jit(solution)/shard_map/forward/pallas_call | solution.py:60
  45.4 86.3 %top.1 = (bf16[512,4096]{1,0:T(8,128)(2,1)}, bf16[512,4096]{1,0:T(8,128)(2,1)}, bf16[4096,512]{1,0:T(8,128)(2,1)}, bf16[2048,512]{1,0:T(8,128)(2,1)}) custom-call(bf16[2048,512]{1,0:T(8,128)(2,1)} %get-tuple-element.20.h_ref, bf16[1,2048,512]{2,1,0:T(8,128)(2,1)} %dy_ref.1, bf16[2,512,4096]{2,1,0:T(8,128)(2,1)} %refs_0_.1, bf16[2,512,4096]{2,1,0:T(8,128)(2,1)} %refs_4_.1, ...), custom_call_target="tpu_custom_call" | custom-call | flops 68719476736 | bytes 41943040 | tf_op jit(solution)/shard_map/top/pallas_call | solution.py:142
  131.7 52.5 %bottom.1 = (bf16[512,4096]{1,0:T(8,128)(2,1)}, bf16[512,4096]{1,0:T(8,128)(2,1)}, bf16[4096,512]{1,0:T(8,128)(2,1)}) custom-call(bf16[2048,512]{1,0:T(8,128)(2,1)} %get-tuple-element.21.dh_ref, bf16[512,2048]{1,0:T(8,128)(2,1)} %get-tuple-element.22.at_ref, f32[2048,4096]{1,0:T(8,128)} %get-tuple-element.23.gate_ref, ...), custom_call_target="tpu_custom_call" | custom-call | flops 34359738368 | bytes 75497472 | tf_op jit(solution)/shard_map/bottom/pallas_call | solution.py:209
  184.2 0.0 all-reduce.3.cloned.1.call-update
  184.2 252.6 %all-reduce.3.cloned.1.call-done = (bf16[1,512,4096]{2,1,0:T(8,128)(2,1)}, bf16[1,512,4096]{2,1,0:T(8,128)(2,1)}, bf16[1,512,4096]{2,1,0:T(8,128)(2,1)}, bf16[1,...) async-done(((bf16[1,512,4096]{2,1,0:T(8,128)(2,1)}, bf16[1,512,4096]{2,1,0:T(8,128)(2,1)}, bf16[1,512,4096]{2,1,0:T(8,128)(2,1)}, ...) | async-done | bytes 25165840 | tf_op jit(solution)/shard_map/psum | solution.py:285
  436.8 0.0 copy-start.4
  436.8 0.0 copy-start.5
  436.8 2.6 constant_dynamic-update-slice_fusion.1
  439.4 0.8 copy-done.4
  440.2 2.2 constant_dynamic-update-slice_fusion.3
  442.5 0.0 copy-done.5
  442.5 4.7 constant_dynamic-update-slice_fusion
  447.2 11.4 %multiply_reduce_fusion.1 = f32[]{:T(128)} fusion(bf16[2,512,4096]{2,1,0:T(8,128)(2,1)} %get-tuple-element.38.refs_7_), kind=kLoop, calls=%fused_computation.1 | loop fusion | flops 12582911 | bytes 8388612 | tf_op jit(solution)/shard_map/reduce_sum | solution.py:287
  458.6 4.9 multiply_reduce_fusion.2
  463.5 0.0 copy-done
  463.5 0.0 copy-done.3
  463.5 0.3 constant_dynamic-update-slice_fusion.5
  463.8 0.0 copy-done.2
  463.8 0.8 constant_dynamic-update-slice_fusion.4.refs_11_
  464.6 0.0 copy-start.1
  464.6 3.2 copy-done.1
  467.8 4.9 multiply_reduce_fusion
  474.7 96.3 %adamw.1 = (bf16[2,512,4096]{2,1,0:T(8,128)(2,1)}, bf16[2,512,4096]{2,1,0:T(8,128)(2,1)}, bf16[2,4096,512]{2,1,0:T(8,128)(2,1)}, f32[2,512,4096]{2,1,0:T(8,128)}...) custom-call(f32[1,1]{1,0:T(1,128)} %bitcast.6.factor_ref, ...), custom_call_target="tpu_custom_call" | custom-call | flops 251658240 | bytes 276824064 | tf_op jit(solution)/shard_map/adamw/pallas_call | solution.py:266
  (3 shorter events, 0.0 us)
Async XLA Ops:
  7.2 429.6 %all-reduce.3.cloned.1.call-start = ((), (), s32[]{:S(2)}) async-start(), calls=%async_computation | async-start | bytes 50331648 | tf_op jit(solution)/shard_map/psum | solution.py:285
  436.8 3.4 copy-start.4
  436.8 5.7 copy-start.5
  447.2 16.3 %copy-start = (bf16[2,512,4096]{2,1,0:T(8,128)(2,1)}, bf16[2,512,4096]{2,1,0:T(8,128)(2,1)S(1)}, u32[]{:S(2)}) copy-start(bf16[2,512,4096]{2,1,0:T(8,128)(2,1)S(1)} %get-tuple-element.37.refs_3_) | copy-start | bytes 25165828
  447.2 16.3 %copy-start.3 = (bf16[1,4096,512]{2,1,0:T(8,128)(2,1)S(1)}, bf16[1,4096,512]{2,1,0:T(8,128)(2,1)}, u32[]{:S(2)}) copy-start(bf16[1,4096,512]{2,1,0:T(8,128)(2,1)} %get-tuple-element.35) | copy-start | bytes 12582916
  458.6 5.2 copy-start.2
  464.6 3.2 copy-start.1
Sparse Core Ops, SparseCore 0:
  184.3 252.4 all-reduce.2

commit v2 on v0

v2 whole, which is shorter than its diff:
```python
import functools
import jax
import jax.numpy as jnp
from jax import lax
from jax.experimental import pallas as pl
from jax.experimental.pallas import tpu as pltpu
from jax.sharding import PartitionSpec as P

F32, BF16 = jnp.float32, jnp.bfloat16
VMEM_LIMIT = 67_000_000


def dot(a, b, da, db):
    return lax.dot_general(a, b, (((da,), (db,)), ((), ())), preferred_element_type=F32)


def norm_scale(wide):
    return lax.rsqrt(jnp.mean(wide * wide, -1, keepdims=True) + 1e-6)


def sigmoid(g):
    return 1.0 / (1.0 + jnp.exp(-g))


def forward_kernel(tb, x_ref, wg_ref, wu_ref, wd_ref, gate_ref, up_ref, h_ref, at_ref, a_ref, acc_ref):
    f, last = pl.program_id(0), pl.num_programs(0) - 1
    tokens = acc_ref.shape[0]

    @pl.when(f == 0)
    def _():
        for t in range(0, tokens, tb):
            rows = pl.ds(t, tb)
            wide = x_ref[0, rows, :].astype(F32)
            a = (wide * norm_scale(wide)).astype(BF16)
            a_ref[rows, :] = a
            at_ref[:, rows] = a.T
            acc_ref[rows, :] = jnp.zeros((tb, acc_ref.shape[1]), F32)

    for t in range(0, tokens, tb):
        rows = pl.ds(t, tb)
        a = a_ref[rows, :]
        gate = dot(a, wg_ref[0], 1, 0)
        up = dot(a, wu_ref[0], 1, 0)
        gate_ref[rows, :] = gate
        up_ref[rows, :] = up
        hid = (gate * sigmoid(gate) * up).astype(BF16)
        acc_ref[rows, :] += dot(hid, wd_ref[0], 1, 0)

    @pl.when(f == last)
    def _():
        for t in range(0, tokens, tb):
            rows = pl.ds(t, tb)
            h_ref[rows, :] = (x_ref[0, rows, :].astype(F32) + acc_ref[rows, :].astype(BF16).astype(F32)).astype(BF16)


def forward(x, wg, wu, wd, fb=256, tb=512):
    _, tokens, d = x.shape
    ff = wg.shape[2]
    whole = lambda *s: pl.BlockSpec(s, lambda f: (0,) * len(s))
    return pl.pallas_call(
        functools.partial(forward_kernel, tb),
        grid=(ff // fb,),
        in_specs=[
            whole(1, tokens, d),
            pl.BlockSpec((1, d, fb), lambda f: (0, 0, f)),
            pl.BlockSpec((1, d, fb), lambda f: (0, 0, f)),
            pl.BlockSpec((1, fb, d), lambda f: (0, f, 0)),
        ],
        out_specs=[
            pl.BlockSpec((tokens, fb), lambda f: (0, f)),
            pl.BlockSpec((tokens, fb), lambda f: (0, f)),
            whole(tokens, d),
            whole(d, tokens),
        ],
        out_shape=[
            jax.ShapeDtypeStruct((tokens, ff), F32),
            jax.ShapeDtypeStruct((tokens, ff), F32),
            jax.ShapeDtypeStruct((tokens, d), BF16),
            jax.ShapeDtypeStruct((d, tokens), BF16),
        ],
        scratch_shapes=[pltpu.VMEM((tokens, d), BF16), pltpu.VMEM((tokens, d), F32)],
        compiler_params=pltpu.CompilerParams(vmem_limit_bytes=VMEM_LIMIT),
        cost_estimate=pl.CostEstimate(flops=6 * tokens * d * ff, bytes_accessed=9 * tokens * ff, transcendentals=0),
        name="forward",
    )(x, wg, wu, wd)


def adamw_kernel(factor_ref, *refs):
    ins, outs = refs[:12], refs[12:]
    factor = factor_ref[0:1, 0:1]
    for i in range(3):
        w, m, v, g = (ins[4 * i + j] for j in range(4))
        g = g[0].astype(F32) * factor
        g = (g.T if i == 2 else g)[None]
        m = 0.9 * m[...] + 0.1 * g
        v = 0.95 * v[...] + 0.05 * g * g
        w = w[...].astype(F32)
        w = w - 0.02 * (m * lax.rsqrt(v + 1e-8) + 0.1 * w)
        outs[i][...] = w.astype(BF16)
        outs[3 + i][...] = m
        outs[6 + i][...] = v


def adamw(factor, ws, ms, vs, gs, steps=16):
    specs = []
    for w in ws:
        layers, r, c = w.shape
        specs.append(pl.BlockSpec((1, r // steps, c), lambda l, f: (l, f, 0)))
    transposed = pl.BlockSpec((1, gs[2].shape[1], gs[2].shape[2] // steps), lambda l, f: (l, 0, f))
    ins, in_specs = [], []
    for i, (w, m, v, g, spec) in enumerate(zip(ws, ms, vs, gs, specs)):
        ins += [w, m, v, g]
        in_specs += [spec] * 3 + [transposed if i == 2 else spec]
    shapes = [jax.ShapeDtypeStruct(w.shape, t) for t in (BF16, F32, F32) for w in ws]
    return pl.pallas_call(
        adamw_kernel,
        grid=(ws[0].shape[0], steps),
        in_specs=[pl.BlockSpec(memory_space=pltpu.VMEM)] + in_specs,
        out_specs=specs * 3,
        out_shape=shapes,
        compiler_params=pltpu.CompilerParams(vmem_limit_bytes=VMEM_LIMIT),
        cost_estimate=pl.CostEstimate(flops=20 * 3 * ws[0].size, bytes_accessed=22 * 3 * ws[0].size, transcendentals=0),
        name="adamw",
    )(factor, *ins)


BLOCK, BLOCKS = 256, 16
WHOLE = 512
ORDERS = ((1, 8, 4, 2), (1, 4, 2, 8), (1, 2, 8, 4))
MATRICES = range(3)


def backward_kernel(tb, gathered, h_ref, dy_ref, a0t_ref, wg_ref, wu_ref, wd_ref, gate_ref, up_ref,
                    g0_ref, g1_ref, g2_ref, factor_ref,
                    a_ref, at_ref, dyt_ref, by_gate, by_up, hid_ref, dgate_ref, dup_ref,
                    keep0, keep1, keep2, keep3, send0, send1, send2, send3, recv0, recv1, recv2, recv3,
                    gbuf, squares, all_squares, rs_send, rs_recv, ag_send, ag_recv, out_sem, in_sem, sq_send, sq_recv):
    t = pl.program_id(0)
    tokens, d = a_ref.shape
    outs = (g0_ref, g1_ref, g2_ref)
    keep, send, recv = (keep0, keep1, keep2, keep3), (send0, send1, send2, send3), (recv0, recv1, recv2, recv3)
    me = lax.axis_index("dp")
    bits = {w: (me // w) % 2 for w in (1, 2, 4, 8)}
    partners = {w: me + w * (1 - 2 * bits[w]) for w in (1, 2, 4, 8)}
    layer = 1 - jnp.minimum(t // BLOCKS, 1)

    def rs_copy(i, m, slot):
        return pltpu.make_async_remote_copy(
            send[i].at[slot, m], recv[i].at[slot, m], rs_send.at[i, m, slot], rs_recv.at[i, m, slot],
            device_id={"dp": partners[ORDERS[m][i]]}, device_id_type=pl.DeviceIdType.MESH)

    def own_rows(m, phase):
        n = WHOLE >> (phase + 1)
        offset = sum(bits[ORDERS[m][q]] * (WHOLE >> (q + 1)) for q in range(phase + 1))
        return pl.ds(pl.multiple_of(offset, n), n)

    def ag_copy(j, m, b):
        part = gbuf.at[m, b % BLOCKS, own_rows(m, 3 - j), :]
        return pltpu.make_async_remote_copy(
            part, part, ag_send.at[j, m, b % 2], ag_recv.at[j, m, b % 2],
            device_id={"dp": partners[ORDERS[m][3 - j]]}, device_id_type=pl.DeviceIdType.MESH)

    def out_copy(m, b):
        columns = pl.ds(pl.multiple_of((b % BLOCKS) * BLOCK, BLOCK), BLOCK)
        return pltpu.make_async_copy(gbuf.at[m, b % BLOCKS], outs[m].at[1 - b // BLOCKS, :, columns], out_sem.at[m, b % 2])

    def half(bit, n):
        return pl.ds(pl.multiple_of(bit * n, n), n)

    @pl.when(t == 0)
    def _():
        first = pltpu.make_async_copy(a0t_ref, at_ref.at[0], in_sem)
        first.start()
        squares[...] = jnp.zeros_like(squares)
        for r in range(0, tokens, tb):
            rows = pl.ds(r, tb)
            wide = h_ref[rows, :].astype(F32)
            a = (wide * norm_scale(wide)).astype(BF16)
            a_ref[rows, :] = a
            at_ref[1, :, rows] = a.T
            dyt_ref[:, rows] = dy_ref[0, rows, :].T
            by_gate[rows, :] = jnp.zeros((tb, d), F32)
            by_up[rows, :] = jnp.zeros((tb, d), F32)
        first.wait()

    @pl.when(t < BLOCKS)
    def _():
        for r in range(0, tokens, tb):
            rows = pl.ds(r, tb)
            a = a_ref[rows, :]
            gate = dot(a, wg_ref[0], 1, 0)
            up = dot(a, wu_ref[0], 1, 0)
            dhid = dot(dy_ref[0, rows, :], wd_ref[0], 1, 1).astype(BF16).astype(F32)
            s = sigmoid(gate)
            silu = gate * s
            hid_ref[rows, :] = (silu * up).astype(BF16)
            dup = (dhid * silu).astype(BF16)
            dgate = (dhid * up * (s + silu * (1.0 - s))).astype(BF16)
            dup_ref[rows, :] = dup
            dgate_ref[rows, :] = dgate
            by_gate[rows, :] += dot(dgate, wg_ref[0], 1, 1)
            by_up[rows, :] += dot(dup, wu_ref[0], 1, 1)

    @pl.when(t == BLOCKS)
    def _():
        for r in range(0, tokens, tb):
            rows = pl.ds(r, tb)
            wide = h_ref[rows, :].astype(F32)
            scale = norm_scale(wide)
            da = (by_gate[rows, :].astype(BF16).astype(F32) + by_up[rows, :].astype(BF16).astype(F32)).astype(BF16).astype(F32)
            dn = scale * da - wide * (scale * scale * scale * jnp.mean(da * wide, -1, keepdims=True))
            dh = (dy_ref[0, rows, :].astype(F32) + dn.astype(BF16).astype(F32)).astype(BF16)
            a_ref[rows, :] = dh
            dyt_ref[:, rows] = dh.T

    @pl.when((t >= BLOCKS) & (t < 2 * BLOCKS))
    def _():
        for r in range(0, tokens, tb):
            rows = pl.ds(r, tb)
            gate, up = gate_ref[rows, :], up_ref[rows, :]
            dhid = dot(a_ref[rows, :], wd_ref[0], 1, 1).astype(BF16).astype(F32)
            s = sigmoid(gate)
            silu = gate * s
            hid_ref[rows, :] = (silu * up).astype(BF16)
            dup_ref[rows, :] = (dhid * silu).astype(BF16)
            dgate_ref[rows, :] = (dhid * up * (s + silu * (1.0 - s))).astype(BF16)

    def active(i):
        return (t >= i) & (t < i + (2 * BLOCKS if i < 5 else gathered))

    for i in (9, 8, 7, 6, 5):
        @pl.when(active(i))
        def _(i=i):
            for m in MATRICES:
                if i == 9:
                    out_copy(m, t - i).wait()
                else:
                    ag_copy(i - 5, m, t - i).wait()

    for i in (4, 3, 2, 1):
        @pl.when(active(i))
        def _(i=i):
            slot = (t - i) % 2
            for m in MATRICES:
                rs_copy(i - 1, m, slot).wait()
            for m in MATRICES:
                if i < 4:
                    n, bit = WHOLE >> (i + 1), bits[ORDERS[m][i]]
                    away, here = half(1 - bit, n), half(bit, n)
                    send[i][slot, m] = (keep[i - 1][m, away, :] + recv[i - 1][slot, m, away, :].astype(F32)).astype(BF16)
                    keep[i][m] = keep[i - 1][m, here, :] + recv[i - 1][slot, m, here, :].astype(F32)
                else:
                    g = (keep[3][m] + recv[3][slot, m].astype(F32)).astype(BF16)
                    gbuf[m, (t - i) % BLOCKS, own_rows(m, 3), :] = g
                    squares[...] += g.astype(F32) * g.astype(F32)

    for i in (8, 7, 6, 5, 4, 3, 2, 1):
        @pl.when(active(i) if i != 4 else (t >= 4) & (t < 4 + gathered))
        def _(i=i):
            for m in MATRICES:
                if i == 8:
                    out_copy(m, t - i).start()
                elif i >= 4:
                    ag_copy(i - 4, m, t - i).start()
                else:
                    rs_copy(i, m, (t - i) % 2).start()

    @pl.when(t < 2 * BLOCKS)
    def _():
        slot = t % 2
        for m, rhs in enumerate((dgate_ref, dup_ref, hid_ref)):
            bit = bits[ORDERS[m][0]]
            away, here = half(1 - bit, WHOLE // 2), half(bit, WHOLE // 2)
            left = (lambda rows: dyt_ref[rows, :]) if m == 2 else (lambda rows: at_ref[layer, rows, :])
            send[0][slot, m] = dot(left(away), rhs[...], 1, 0).astype(BF16)
            keep[0][m] = dot(left(here), rhs[...], 1, 0)
            rs_copy(0, m, slot).start()

    others = range(1, 16)

    def square_copy(k, row):
        return pltpu.make_async_remote_copy(
            all_squares.at[me], all_squares.at[row], sq_send.at[k], sq_recv.at[k],
            device_id={"dp": (me + k) % 16}, device_id_type=pl.DeviceIdType.MESH)

    @pl.when(t == 2 * BLOCKS + 4)
    def _():
        total = squares[0:8, :]
        for r in range(8, squares.shape[0], 8):
            total = total + squares[r : r + 8, :]
        all_squares[me] = total[:, :128] + total[:, 128:]
        for k in others:
            square_copy(k, me).start()

    @pl.when(t == pl.num_programs(0) - 1)
    def _():
        for k in others:
            copy = square_copy(k, (me + 16 - k) % 16)
            copy.wait_send()
            copy.wait_recv()
        total = all_squares[0]
        for k in others:
            total = total + all_squares[k]
        count = 2 * 3 * WHOLE * BLOCK * BLOCKS
        factor = jnp.minimum(1.0, 0.5 * lax.rsqrt(jnp.sum(total, keepdims=True) / count + 1e-30))
        factor_ref[...] = jnp.broadcast_to(factor, factor_ref.shape)


def backward(h, dy, a0t, ws, gate, up, gathered=2 * BLOCKS, tb=512):
    tokens, d = h.shape
    ff = gate.shape[1]
    assert (d, ff) == (WHOLE, BLOCK * BLOCKS)
    vmem = pl.BlockSpec(memory_space=pltpu.VMEM)
    anywhere = pl.BlockSpec(memory_space=pl.ANY)
    top_block = lambda t: (1, 0, jnp.minimum(t, BLOCKS - 1))
    low_block = lambda t: (0, jnp.minimum(jnp.maximum(t - BLOCKS, 0), BLOCKS - 1))

    def down_block(t):
        t = jnp.minimum(t, 2 * BLOCKS - 1)
        return (1 - t // BLOCKS, t % BLOCKS, 0)

    sizes = [WHOLE >> (i + 1) for i in range(4)]
    return pl.pallas_call(
        functools.partial(backward_kernel, tb, gathered),
        grid=(2 * BLOCKS + max(gathered - 2 * BLOCKS + 9, 6),),
        in_specs=[
            vmem, vmem, anywhere,
            pl.BlockSpec((1, d, BLOCK), top_block),
            pl.BlockSpec((1, d, BLOCK), top_block),
            pl.BlockSpec((1, BLOCK, d), down_block),
            pl.BlockSpec((tokens, BLOCK), low_block),
            pl.BlockSpec((tokens, BLOCK), low_block),
        ],
        out_specs=[anywhere] * 3 + [vmem],
        out_shape=[jax.ShapeDtypeStruct((2, WHOLE, ff), BF16)] * 3 + [jax.ShapeDtypeStruct((8, 128), F32)],
        scratch_shapes=[
            pltpu.VMEM((tokens, d), BF16),
            pltpu.VMEM((2, d, tokens), BF16),
            pltpu.VMEM((d, tokens), BF16),
            pltpu.VMEM((tokens, d), F32),
            pltpu.VMEM((tokens, d), F32),
            pltpu.VMEM((tokens, BLOCK), BF16),
            pltpu.VMEM((tokens, BLOCK), BF16),
            pltpu.VMEM((tokens, BLOCK), BF16),
            *[pltpu.VMEM((3, n, BLOCK), F32) for n in sizes],
            *[pltpu.VMEM((2, 3, n, BLOCK), BF16) for n in sizes],
            *[pltpu.VMEM((2, 3, n, BLOCK), BF16) for n in sizes],
            pltpu.VMEM((3, BLOCKS, WHOLE, BLOCK), BF16),
            pltpu.VMEM((sizes[3], BLOCK), F32),
            pltpu.VMEM((16, 8, 128), F32),
            pltpu.SemaphoreType.DMA((4, 3, 2)),
            pltpu.SemaphoreType.DMA((4, 3, 2)),
            pltpu.SemaphoreType.DMA((4, 3, 2)),
            pltpu.SemaphoreType.DMA((4, 3, 2)),
            pltpu.SemaphoreType.DMA((3, 2)),
            pltpu.SemaphoreType.DMA,
            pltpu.SemaphoreType.DMA((16,)),
            pltpu.SemaphoreType.DMA((16,)),
        ],
        compiler_params=pltpu.CompilerParams(vmem_limit_bytes=VMEM_LIMIT, has_side_effects=True),
        cost_estimate=pl.CostEstimate(flops=24 * tokens * d * ff, bytes_accessed=12 * tokens * ff, transcendentals=0),
        name="backward",
    )(h, dy, a0t, *ws, gate, up)


def solution(mesh):
    def step(x, dy, *arrays):
        ws, ms, vs = (arrays[i : i + 3] for i in (0, 3, 6))
        gate, up, h, at = forward(x, *ws)
        *gs, factor = backward(h, dy, at, ws, gate, up)
        return tuple(adamw(factor, ws, ms, vs, gs))

    return jax.shard_map(
        step,
        mesh=mesh,
        in_specs=(P(("rep", "dp"), None, None),) * 2 + (P(None, None, None),) * 9,
        out_specs=(P("rep", None, None),) * 9,
        check_vma=False,
    )
```

time: 710 us -> 365 us (0.51); the launches traced: 702 us -> 365 us
  Pallas kernels: 0 us -> 364 us
  matrix products: 318 us -> 0 us
  waiting for transfers between devices: 253 us -> 0 us
  other arithmetic: 108 us -> 0 us
  between operations: 16.4 us -> 0.81 us
  local copies, waits for them, and re-layouts: 7.17 us -> 0 us
    pallas_call x0 -> x3, Pallas kernels: none -> 364 us  [the longest x1 231 us: backward(): pl.pallas_call(functools.partial(backward_kernel, tb, gathered), grid=(2...]
    dot_general x15 -> x0, matrix products: 318 us -> none  [the longest x5 118 us: layer(): gate = jnp.dot(a, w['w_gate'], preferred_element_type=jnp.float32)]
    psum x1 -> x0, waiting for transfers between devices: 253 us -> none  [step(): summed[number] = [lax.psum(by_w[name], 'dp') for name in NAMES]]
    convert_element_type x2 -> x0, other arithmetic: 86.6 us -> none  [adamw(): return ((w - 0.02 * step).astype(jnp.bfloat16), m, v)]
    reduce_sum x4 -> x0, other arithmetic: 20.2 us -> none  [the longest x3 19.8 us: step(): jnp.sum(g * g)]
    unnamed x36 -> x0, local copies, waits for them, and re-layouts: 7.17 us -> none
  transfers between devices with their start and end apart: 1 -> 0, of which waited for: 1 -> 0; matrix products, arithmetic and copies ran while one was open for 0% -> 0% of each run, Pallas kernels for 0% -> 0%
where the time goes in v2:
time: 365 us
  Pallas kernels  364 us (100%)
    pallas_call x1, Pallas kernels, backward(): pl.pallas_call(functools.partial(backward_kernel, tb, gathered), grid=(2...  231 us
    pallas_call x1, Pallas kernels, adamw(): pl.pallas_call(adamw_kernel, grid=(ws[0].shape[0], steps), in_specs=[pl.B...  95.6 us
    pallas_call x1, Pallas kernels, forward(): pl.pallas_call(functools.partial(forward_kernel, tb), grid=(ff // fb,), i...  37.5 us

profile of v2, /device:TPU:0, one launch (start us, length us, event | category | flops | bytes accessed | tf_op | source)
XLA Modules:
  0.0 365.1 jit_solution(7068366413050509692)
XLA Ops:
  0.6 37.5 %forward.1 = (f32[2048,4096]{1,0:T(8,128)}, f32[2048,4096]{1,0:T(8,128)}, bf16[2048,512]{1,0:T(8,128)(2,1)}, bf16[512,2048]{1,0:T(8,128)(2,1)}) custom-call(bf16[1,2048,512]{2,1,0:T(8,128)(2,1)} %x_ref.1, bf16[2,512,4096]{2,1,0:T(8,128)(2,1)} %refs_0_.1, bf16[2,512,4096]{2,1,0:T(8,128)(2,1)} %refs_4_.1, bf16[2,4096,512]{2,1,0:T(8,128)(2,1)} %refs_8_.1), custom_call_target="tpu_custom_call" | custom-call | flops 25769803776 | bytes 75497472 | tf_op jit(solution)/shard_map/forward/pallas_call | solution.py:60
  38.2 231.1 %backward.1 = (bf16[2,512,4096]{2,1,0:T(8,128)(2,1)}, bf16[2,512,4096]{2,1,0:T(8,128)(2,1)}, bf16[2,512,4096]{2,1,0:T(8,128)(2,1)}, f32[8,128]{1,0:T(8,128)}) custom-call(bf16[2048,512]{1,0:T(8,128)(2,1)} %get-tuple-element.17.h_ref, bf16[1,2048,512]{2,1,0:T(8,128)(2,1)} %dy_ref.1, bf16[512,2048]{1,0:T(8,128)(2,1)} %get-tuple-element.18.a0t_ref, ...), custom_call_target="tpu_custom_call" | custom-call | flops 103079215104 | bytes 100663296 | tf_op jit(solution)/shard_map/backward/pallas_call | solution.py:323
  269.3 95.6 %adamw.1 = (bf16[2,512,4096]{2,1,0:T(8,128)(2,1)}, bf16[2,512,4096]{2,1,0:T(8,128)(2,1)}, bf16[2,4096,512]{2,1,0:T(8,128)(2,1)}, f32[2,512,4096]{2,1,0:T(8,128)}...) custom-call(f32[8,128]{1,0:T(8,128)} %get-tuple-element.21.factor_re, ...), custom_call_target="tpu_custom_call" | custom-call | flops 251658240 | bytes 276824064 | tf_op jit(solution)/shard_map/adamw/pallas_call | solution.py:115

commit v3 on v2

--- a/solution.py
+++ b/solution.py
@@ -22,7 +22,17 @@
     return 1.0 / (1.0 + jnp.exp(-g))
 
 
-def forward_kernel(tb, x_ref, wg_ref, wu_ref, wd_ref, gate_ref, up_ref, h_ref, at_ref, a_ref, acc_ref):
+def interleave(n, first, second, third):
+    for r in range(n + 2):
+        if r < n:
+            first(r)
+        if 0 <= r - 2:
+            third(r - 2)
+        if 0 <= r - 1 < n:
+            second(r - 1)
+
+
+def forward_kernel(tb, x_ref, wg_ref, wu_ref, wd_ref, gate_ref, up_ref, h_ref, at_ref, a_ref, acc_ref, hid_ref):
     f, last = pl.program_id(0), pl.num_programs(0) - 1
     tokens = acc_ref.shape[0]
 
@@ -36,15 +46,21 @@
             at_ref[:, rows] = a.T
             acc_ref[rows, :] = jnp.zeros((tb, acc_ref.shape[1]), F32)
 
-    for t in range(0, tokens, tb):
-        rows = pl.ds(t, tb)
-        a = a_ref[rows, :]
-        gate = dot(a, wg_ref[0], 1, 0)
-        up = dot(a, wu_ref[0], 1, 0)
-        gate_ref[rows, :] = gate
-        up_ref[rows, :] = up
-        hid = (gate * sigmoid(gate) * up).astype(BF16)
-        acc_ref[rows, :] += dot(hid, wd_ref[0], 1, 0)
+    def project(r):
+        rows = pl.ds(r * tb, tb)
+        gate_ref[rows, :] = dot(a_ref[rows, :], wg_ref[0], 1, 0)
+        up_ref[rows, :] = dot(a_ref[rows, :], wu_ref[0], 1, 0)
+
+    def product(r):
+        rows = pl.ds(r * tb, tb)
+        gate = gate_ref[rows, :]
+        hid_ref[rows, :] = (gate * sigmoid(gate) * up_ref[rows, :]).astype(BF16)
+
+    def down(r):
+        rows = pl.ds(r * tb, tb)
+        acc_ref[rows, :] += dot(hid_ref[rows, :], wd_ref[0], 1, 0)
+
+    interleave(tokens // tb, project, product, down)
 
     @pl.when(f == last)
     def _():
@@ -78,7 +94,7 @@
             jax.ShapeDtypeStruct((tokens, d), BF16),
             jax.ShapeDtypeStruct((d, tokens), BF16),
         ],
-        scratch_shapes=[pltpu.VMEM((tokens, d), BF16), pltpu.VMEM((tokens, d), F32)],
+        scratch_shapes=[pltpu.VMEM((tokens, d), BF16), pltpu.VMEM((tokens, d), F32), pltpu.VMEM((tokens, fb), BF16)],
         compiler_params=pltpu.CompilerParams(vmem_limit_bytes=VMEM_LIMIT),
         cost_estimate=pl.CostEstimate(flops=6 * tokens * d * ff, bytes_accessed=9 * tokens * ff, transcendentals=0),
         name="forward",
@@ -101,7 +117,7 @@
         outs[6 + i][...] = v
 
 
-def adamw(factor, ws, ms, vs, gs, steps=16):
+def adamw(factor, ws, ms, vs, gs, steps=8):
     specs = []
     for w in ws:
         layers, r, c = w.shape
@@ -130,19 +146,18 @@
 MATRICES = range(3)
 
 
-def backward_kernel(tb, gathered, h_ref, dy_ref, a0t_ref, wg_ref, wu_ref, wd_ref, gate_ref, up_ref,
+def backward_kernel(tb, h_ref, dy_ref, a0t_ref, wg_ref, wu_ref, wd_ref, gate_ref, up_ref,
                     g0_ref, g1_ref, g2_ref, factor_ref,
-                    a_ref, at_ref, dyt_ref, by_gate, by_up, hid_ref, dgate_ref, dup_ref,
-                    keep0, keep1, keep2, keep3, send0, send1, send2, send3, recv0, recv1, recv2, recv3,
+                    a_ref, at_ref, dyt_ref, by_gate, by_up, hid_ref, dgate_ref, dup_ref, gate_buf, up_buf, dhid_buf,
+                    own_term, keep1, keep2, keep3, send0, send1, send2, send3, recv0, recv1, recv2, recv3,
                     gbuf, squares, all_squares, rs_send, rs_recv, ag_send, ag_recv, out_sem, in_sem, sq_send, sq_recv):
     t = pl.program_id(0)
     tokens, d = a_ref.shape
     outs = (g0_ref, g1_ref, g2_ref)
-    keep, send, recv = (keep0, keep1, keep2, keep3), (send0, send1, send2, send3), (recv0, recv1, recv2, recv3)
+    keep, send, recv = (None, keep1, keep2, keep3), (send0, send1, send2, send3), (recv0, recv1, recv2, recv3)
     me = lax.axis_index("dp")
     bits = {w: (me // w) % 2 for w in (1, 2, 4, 8)}
     partners = {w: me + w * (1 - 2 * bits[w]) for w in (1, 2, 4, 8)}
-    layer = 1 - jnp.minimum(t // BLOCKS, 1)
 
     def rs_copy(i, m, slot):
         return pltpu.make_async_remote_copy(
@@ -183,24 +198,6 @@
             by_up[rows, :] = jnp.zeros((tb, d), F32)
         first.wait()
 
-    @pl.when(t < BLOCKS)
-    def _():
-        for r in range(0, tokens, tb):
-            rows = pl.ds(r, tb)
-            a = a_ref[rows, :]
-            gate = dot(a, wg_ref[0], 1, 0)
-            up = dot(a, wu_ref[0], 1, 0)
-            dhid = dot(dy_ref[0, rows, :], wd_ref[0], 1, 1).astype(BF16).astype(F32)
-            s = sigmoid(gate)
-            silu = gate * s
-            hid_ref[rows, :] = (silu * up).astype(BF16)
-            dup = (dhid * silu).astype(BF16)
-            dgate = (dhid * up * (s + silu * (1.0 - s))).astype(BF16)
-            dup_ref[rows, :] = dup
-            dgate_ref[rows, :] = dgate
-            by_gate[rows, :] += dot(dgate, wg_ref[0], 1, 1)
-            by_up[rows, :] += dot(dup, wu_ref[0], 1, 1)
-
     @pl.when(t == BLOCKS)
     def _():
         for r in range(0, tokens, tb):
@@ -213,68 +210,102 @@
             a_ref[rows, :] = dh
             dyt_ref[:, rows] = dh.T
 
+    def wait_and_add(i):
+        b = t - i
+        slot = b % 2
+        for m in MATRICES:
+            if 2 <= i <= 5:
+                rs_copy(i - 2, m, slot).wait()
+            elif 6 <= i <= 9:
+                ag_copy(i - 6, m, b).wait()
+            elif i == 10:
+                out_copy(m, b).wait()
+        for m in MATRICES:
+            if i == 1:
+                send[0][slot, m] = own_term[slot, m, half(1 - bits[ORDERS[m][0]], WHOLE // 2), :].astype(BF16)
+            elif i < 5:
+                n, bit = WHOLE >> i, bits[ORDERS[m][i - 1]]
+                away, here = half(1 - bit, n), half(bit, n)
+                if i == 2:
+                    base = bits[ORDERS[m][0]] * 2
+                    mine = own_term[slot, m, half(base + 1 - bit, n), :], own_term[slot, m, half(base + bit, n), :]
+                else:
+                    mine = keep[i - 2][m, away, :], keep[i - 2][m, here, :]
+                send[i - 1][slot, m] = (mine[0] + recv[i - 2][slot, m, away, :].astype(F32)).astype(BF16)
+                keep[i - 1][m] = mine[1] + recv[i - 2][slot, m, here, :].astype(F32)
+            elif i == 5:
+                g = (keep[3][m] + recv[3][slot, m].astype(F32)).astype(BF16)
+                gbuf[m, b % BLOCKS, own_rows(m, 3), :] = g
+                squares[...] += g.astype(F32) * g.astype(F32)
+
+    def start(i):
+        for m in MATRICES:
+            if i <= 4:
+                rs_copy(i - 1, m, (t - i) % 2).start()
+            elif i <= 8:
+                ag_copy(i - 5, m, t - i).start()
+            elif i == 9:
+                out_copy(m, t - i).start()
+
+    steady = (t >= 10) & (t < 2 * BLOCKS + 1)
+
+    @pl.when(steady)
+    def _():
+        for i in range(10, 0, -1):
+            wait_and_add(i)
+        for i in range(9, 0, -1):
+            start(i)
+
+    @pl.when(jnp.logical_not(steady))
+    def _():
+        for act in (wait_and_add, start):
+            for i in range(10, 0, -1):
+                pl.when((t >= i) & (t < i + 2 * BLOCKS))(functools.partial(act, i))
+
+    def elementwise(r, gate, up, dhid):
+        rows = pl.ds(r * tb, tb)
+        dhid = dhid.astype(BF16).astype(F32)
+        s = sigmoid(gate)
+        silu = gate * s
+        hid_ref[rows, :] = (silu * up).astype(BF16)
+        dup_ref[rows, :] = (dhid * silu).astype(BF16)
+        dgate_ref[rows, :] = (dhid * up * (s + silu * (1.0 - s))).astype(BF16)
+
+    def weight_terms(r, which):
+        rows = pl.ds(r * tb, tb)
+        for m, rhs in enumerate((dgate_ref, dup_ref, hid_ref)):
+            term = dot(dyt_ref[:, rows] if m == 2 else at_ref[which, :, rows], rhs[rows, :], 1, 0)
+            own_term[t % 2, m] = term if r == 0 else own_term[t % 2, m] + term
+
+    @pl.when(t < BLOCKS)
+    def _():
+        def first(r):
+            rows = pl.ds(r * tb, tb)
+            gate_buf[r % 2] = dot(a_ref[rows, :], wg_ref[0], 1, 0)
+            up_buf[r % 2] = dot(a_ref[rows, :], wu_ref[0], 1, 0)
+            dhid_buf[r % 2] = dot(dy_ref[0, rows, :], wd_ref[0], 1, 1)
+
+        def second(r):
+            elementwise(r, gate_buf[r % 2], up_buf[r % 2], dhid_buf[r % 2])
+
+        def third(r):
+            rows = pl.ds(r * tb, tb)
+            by_gate[rows, :] += dot(dgate_ref[rows, :], wg_ref[0], 1, 1)
+            by_up[rows, :] += dot(dup_ref[rows, :], wu_ref[0], 1, 1)
+            weight_terms(r, 1)
+
+        interleave(tokens // tb, first, second, third)
+
     @pl.when((t >= BLOCKS) & (t < 2 * BLOCKS))
     def _():
-        for r in range(0, tokens, tb):
-            rows = pl.ds(r, tb)
-            gate, up = gate_ref[rows, :], up_ref[rows, :]
-            dhid = dot(a_ref[rows, :], wd_ref[0], 1, 1).astype(BF16).astype(F32)
-            s = sigmoid(gate)
-            silu = gate * s
-            hid_ref[rows, :] = (silu * up).astype(BF16)
-            dup_ref[rows, :] = (dhid * silu).astype(BF16)
-            dgate_ref[rows, :] = (dhid * up * (s + silu * (1.0 - s))).astype(BF16)
-
-    def active(i):
-        return (t >= i) & (t < i + (2 * BLOCKS if i < 5 else gathered))
-
-    for i in (9, 8, 7, 6, 5):
-        @pl.when(active(i))
-        def _(i=i):
-            for m in MATRICES:
-                if i == 9:
-                    out_copy(m, t - i).wait()
-                else:
-                    ag_copy(i - 5, m, t - i).wait()
-
-    for i in (4, 3, 2, 1):
-        @pl.when(active(i))
-        def _(i=i):
-            slot = (t - i) % 2
-            for m in MATRICES:
-                rs_copy(i - 1, m, slot).wait()
-            for m in MATRICES:
-                if i < 4:
-                    n, bit = WHOLE >> (i + 1), bits[ORDERS[m][i]]
-                    away, here = half(1 - bit, n), half(bit, n)
-                    send[i][slot, m] = (keep[i - 1][m, away, :] + recv[i - 1][slot, m, away, :].astype(F32)).astype(BF16)
-                    keep[i][m] = keep[i - 1][m, here, :] + recv[i - 1][slot, m, here, :].astype(F32)
-                else:
-                    g = (keep[3][m] + recv[3][slot, m].astype(F32)).astype(BF16)
-                    gbuf[m, (t - i) % BLOCKS, own_rows(m, 3), :] = g
-                    squares[...] += g.astype(F32) * g.astype(F32)
-
-    for i in (8, 7, 6, 5, 4, 3, 2, 1):
-        @pl.when(active(i) if i != 4 else (t >= 4) & (t < 4 + gathered))
-        def _(i=i):
-            for m in MATRICES:
-                if i == 8:
-                    out_copy(m, t - i).start()
-                elif i >= 4:
-                    ag_copy(i - 4, m, t - i).start()
-                else:
-                    rs_copy(i, m, (t - i) % 2).start()
-
-    @pl.when(t < 2 * BLOCKS)
-    def _():
-        slot = t % 2
-        for m, rhs in enumerate((dgate_ref, dup_ref, hid_ref)):
-            bit = bits[ORDERS[m][0]]
-            away, here = half(1 - bit, WHOLE // 2), half(bit, WHOLE // 2)
-            left = (lambda rows: dyt_ref[rows, :]) if m == 2 else (lambda rows: at_ref[layer, rows, :])
-            send[0][slot, m] = dot(left(away), rhs[...], 1, 0).astype(BF16)
-            keep[0][m] = dot(left(here), rhs[...], 1, 0)
-            rs_copy(0, m, slot).start()
+        def first(r):
+            dhid_buf[r % 2] = dot(a_ref[pl.ds(r * tb, tb), :], wd_ref[0], 1, 1)
+
+        def second(r):
+            rows = pl.ds(r * tb, tb)
+            elementwise(r, gate_ref[rows, :], up_ref[rows, :], dhid_buf[r % 2])
+
+        interleave(tokens // tb, first, second, lambda r: weight_terms(r, 0))
 
     others = range(1, 16)
 
@@ -283,7 +314,7 @@
             all_squares.at[me], all_squares.at[row], sq_send.at[k], sq_recv.at[k],
             device_id={"dp": (me + k) % 16}, device_id_type=pl.DeviceIdType.MESH)
 
-    @pl.when(t == 2 * BLOCKS + 4)
+    @pl.when(t == 2 * BLOCKS + 5)
     def _():
         total = squares[0:8, :]
         for r in range(8, squares.shape[0], 8):
@@ -306,7 +337,7 @@
         factor_ref[...] = jnp.broadcast_to(factor, factor_ref.shape)
 
 
-def backward(h, dy, a0t, ws, gate, up, gathered=2 * BLOCKS, tb=512):
+def backward(h, dy, a0t, ws, gate, up, tb=512):
     tokens, d = h.shape
     ff = gate.shape[1]
     assert (d, ff) == (WHOLE, BLOCK * BLOCKS)
@@ -321,8 +352,8 @@
 
     sizes = [WHOLE >> (i + 1) for i in range(4)]
     return pl.pallas_call(
-        functools.partial(backward_kernel, tb, gathered),
-        grid=(2 * BLOCKS + max(gathered - 2 * BLOCKS + 9, 6),),
+        functools.partial(backward_kernel, tb),
+        grid=(2 * BLOCKS + 10,),
         in_specs=[
             vmem, vmem, anywhere,
             pl.BlockSpec((1, d, BLOCK), top_block),
@@ -342,7 +373,9 @@
             pltpu.VMEM((tokens, BLOCK), BF16),
             pltpu.VMEM((tokens, BLOCK), BF16),
             pltpu.VMEM((tokens, BLOCK), BF16),
-            *[pltpu.VMEM((3, n, BLOCK), F32) for n in sizes],
+            *[pltpu.VMEM((2, tb, BLOCK), F32)] * 3,
+            pltpu.VMEM((2, 3, WHOLE, BLOCK), F32),
+            *[pltpu.VMEM((3, n, BLOCK), F32) for n in sizes[1:]],
             *[pltpu.VMEM((2, 3, n, BLOCK), BF16) for n in sizes],
             *[pltpu.VMEM((2, 3, n, BLOCK), BF16) for n in sizes],
             pltpu.VMEM((3, BLOCKS, WHOLE, BLOCK), BF16),

time: 365 us -> 365 us (level)
    pallas_call x1, Pallas kernels: 231 us -> 238 us  [backward(): pl.pallas_call(functools.partial(backward_kernel, tb), grid=(2 * BLOCKS +...]
    pallas_call x1, Pallas kernels: 95.6 us -> 88.5 us  [adamw(): pl.pallas_call(adamw_kernel, grid=(ws[0].shape[0], steps), in_specs=[pl.B...]
where the time goes in v3:
time: 365 us
  Pallas kernels  364 us (100%)
    pallas_call x1, Pallas kernels, backward(): pl.pallas_call(functools.partial(backward_kernel, tb), grid=(2 * BLOCKS +...  238 us
    pallas_call x1, Pallas kernels, adamw(): pl.pallas_call(adamw_kernel, grid=(ws[0].shape[0], steps), in_specs=[pl.B...  88.5 us
    pallas_call x1, Pallas kernels, forward(): pl.pallas_call(functools.partial(forward_kernel, tb), grid=(ff // fb,), i...  37.6 us

profile of v3, /device:TPU:0, one launch (start us, length us, event | category | flops | bytes accessed | tf_op | source)
XLA Modules:
  0.0 365.3 jit_solution(142073369619582825)
XLA Ops:
  0.6 37.6 %forward.1 = (f32[2048,4096]{1,0:T(8,128)}, f32[2048,4096]{1,0:T(8,128)}, bf16[2048,512]{1,0:T(8,128)(2,1)}, bf16[512,2048]{1,0:T(8,128)(2,1)}) custom-call(bf16[1,2048,512]{2,1,0:T(8,128)(2,1)} %x_ref.1, bf16[2,512,4096]{2,1,0:T(8,128)(2,1)} %refs_0_.1, bf16[2,512,4096]{2,1,0:T(8,128)(2,1)} %refs_4_.1, bf16[2,4096,512]{2,1,0:T(8,128)(2,1)} %refs_8_.1), custom_call_target="tpu_custom_call" | custom-call | flops 25769803776 | bytes 75497472 | tf_op jit(solution)/shard_map/forward/pallas_call | solution.py:76
  38.2 238.4 %backward.1 = (bf16[2,512,4096]{2,1,0:T(8,128)(2,1)}, bf16[2,512,4096]{2,1,0:T(8,128)(2,1)}, bf16[2,512,4096]{2,1,0:T(8,128)(2,1)}, f32[8,128]{1,0:T(8,128)}) custom-call(bf16[2048,512]{1,0:T(8,128)(2,1)} %get-tuple-element.17.h_ref, bf16[1,2048,512]{2,1,0:T(8,128)(2,1)} %dy_ref.1, bf16[512,2048]{1,0:T(8,128)(2,1)} %get-tuple-element.18.a0t_ref, ...), custom_call_target="tpu_custom_call" | custom-call | flops 103079215104 | bytes 100663296 | tf_op jit(solution)/shard_map/backward/pallas_call | solution.py:354
  276.6 88.5 %adamw.1 = (bf16[2,512,4096]{2,1,0:T(8,128)(2,1)}, bf16[2,512,4096]{2,1,0:T(8,128)(2,1)}, bf16[2,4096,512]{2,1,0:T(8,128)(2,1)}, f32[2,512,4096]{2,1,0:T(8,128)}...) custom-call(f32[8,128]{1,0:T(8,128)} %get-tuple-element.21.factor_re, ...), custom_call_target="tpu_custom_call" | custom-call | flops 251658240 | bytes 276824064 | tf_op jit(solution)/shard_map/adamw/pallas_call | solution.py:131
